TPU v7x, 128 devices: a whole 4x4x4 slice. The times are simulated.
128 devices in a mesh: px: 8 (over y_hi, z), py: 16 (over y_lo, x, core).
Axes of the slice: x: 4, y: 4 (y_hi: 2, y_lo: 2; y = y_hi * 2 + y_lo), z: 4, core: 2. Of those that a mesh axis runs over, the one named last changes fastest.
Arguments:
- vorticity: float32 [3, 192, 36864], P(None, 'px', 'py'), may hold values from -6 to 6
Outputs:
- velocity: float32 [3, 192, 36864], P(None, 'px', 'py')
- stretching: float32 [3, 192, 36864], P(None, 'px', 'py')
All inputs are finite; a program needn't handle non-finite values.
Results may differ from a plain program's by a relative error of at most 0.0003.
Values sent between devices are 32-bit elements; how exact they have to be, the bound alone decides.
A program may use at most 128 MiB of HBM per device.

v0:
```python
import math
import functools

import numpy as np
import jax
import jax.numpy as jnp
from jax import lax
from jax.experimental import pallas as pl
from jax.experimental.pallas import tpu as pltpu
from jax.sharding import PartitionSpec as P

G = 192
N = 2 * G
MESH = pl.DeviceIdType.MESH
VMEM = pltpu.VMEM
ANY = pl.ANY
bf16 = jnp.bfloat16
f32 = jnp.float32


def pair_np(t):
    hi = np.asarray(t, np.float32).astype(jnp.bfloat16)
    lo = (t - hi.astype(np.float64)).astype(np.float32).astype(jnp.bfloat16)
    return hi, lo


def trig(m, t, j):
    a = 2.0 * np.pi * ((m * j) % N) / N
    return np.where(t == 0, np.cos(a), np.sin(a))


def weight(m):
    return np.where(m == 0, 1.0, 2.0) / N


def tables():
    r = np.arange(384)
    dg, zm, dl = r // 48, (r // 8) % 6, r % 8
    mz, tz = 3 * (8 * dg + dl) + zm // 2, zm % 2
    z = np.arange(256)
    zf = np.where(z[None] < G, trig(mz[:, None], tz[:, None], z[None]), 0.0)
    zi = (zf * weight(mz)[:, None]).T.reshape(256, 8, 3, 2, 8).transpose(2, 0, 1, 3, 4).reshape(3, 256, 128)
    my, ty = 2 * (r % 96) + r // 192, (r // 96) % 2
    k = np.arange(192)
    jy = 12 * (k % 16) + k // 16
    yf = trig(my[:, None], ty[:, None], jy[None])
    yi = (yf * weight(my)[:, None]).T
    mx, tx = 64 * (r // 128) + r % 64, (r // 64) % 2
    lane = np.arange(128)
    jx = 96 * np.arange(2)[:, None] + lane[None]
    xf = np.where(lane[None, :, None] < 96, trig(mx[None, None], tx[None, None], jx[:, :, None]), 0.0)
    xi = np.swapaxes(xf * weight(mx)[None, None], 1, 2)
    stack = lambda t: np.stack(pair_np(t), axis=-3)
    wide = lambda t: np.concatenate([pair_np(t)[0], pair_np(t)[0], pair_np(t)[1]], axis=-1)
    return [stack(zf), wide(yf), stack(xf), stack(xi), wide(yi), stack(zi)]


def split(x):
    hi = x.astype(bf16)
    lo = (x - hi.astype(f32)).astype(bf16)
    return hi, lo


def cat(parts, axis):
    return jnp.concatenate(parts, axis=axis)


def lanes(shape):
    return lax.broadcasted_iota(jnp.int32, shape, len(shape) - 1)


def dot(a, b, rhs_t=False):
    return lax.dot_general(a, b, (((1,), (1 if rhs_t else 0,)), ((), ())), preferred_element_type=f32)


def padded_line(vort, c, y, lane):
    a, b, d = [vort[c, :, pl.ds(384 * (y // 2) + 128 * i, 128)] for i in range(3)]
    if y % 2 == 0:
        return a, jnp.where(lane < 64, b, 0.0)
    rb, rd = pltpu.roll(b, 64, 1), pltpu.roll(d, 64, 1)
    return jnp.where(lane < 64, rb, rd), jnp.where(lane < 64, rd, 0.0)


def z_forward(vort, zf, out, w):
    lane = lanes((24, 128))
    for y in range(12):
        for c in range(3):
            v0, v1 = padded_line(vort, c, y, lane)
            r0 = y * 72 + c * 24
            w[pl.ds(r0, 24), pl.ds(0, 128)] = v0
            w[pl.ds(r0, 24), pl.ds(128, 128)] = v1
    w[pl.ds(864, 32), :] = jnp.zeros((32, 256), f32)
    table = cat([zf[0], zf[0], zf[1]], 1)
    for blk, n in ((0, 256), (256, 256), (512, 256), (768, 128)):
        hi, lo = split(w[pl.ds(blk, n), :])
        acc = dot(table, cat([hi, lo, hi], 1), rhs_t=True)
        for jj in range(n // 128):
            out[:, :, blk // 128 + jj] = acc[:, 128 * jj : 128 * jj + 128].reshape(8, 6, 8, 128)


def y_forward(zm, r, ty, out, s):
    lane = lanes((8, 128))
    zero = jnp.zeros((8, 128), f32)
    for y in range(12):
        for c in range(3):
            j, o = divmod(24 * (3 * y + c), 128)
            for qh in range(2):
                v = zero
                for pp in (3, 2, 1, 0):
                    t = r[zm, pp, qh, j]
                    if o + 24 > 128:
                        t = jnp.where(lane >= o, t, r[zm, pp, qh, j + 1])
                    t = pltpu.roll(t, (24 * pp - o) % 128, 1)
                    v = jnp.where(lane < 24 * pp + 24, t, v)
                s[pl.ds(8 * (2 * y + qh), 8), pl.ds(128 * c, 128)] = v
    hi, lo = split(s[...])
    acc = dot(ty[...], cat([hi, lo, hi], 0))
    for h in range(2):
        for c in range(3):
            out[h, 3 * zm + c] = acc[192 * h : 192 * h + 192, 128 * c : 128 * c + 128]


def green_table(chip, core, out):
    unit = 2.0 * math.pi / N
    lane = lanes((8, 128))
    row = lax.broadcasted_iota(jnp.int32, (8, 128), 0)

    def body(it, _):
        kz = (3 * chip + it // 12).astype(f32) * unit
        ky = (16 * (it % 12) + core + 2 * row).astype(f32) * unit
        for tl in range(3):
            kx = (64 * tl + lane % 64).astype(f32) * unit
            sq = kx * kx + ky * ky + kz * kz
            green = jnp.exp(-0.5 * sq) / (sq + jnp.where(sq == 0.0, 1.0, 0.0))
            out[pl.ds(pl.multiple_of(8 * it, 8), 8), pl.ds(128 * tl, 128)] = green
        return 0

    lax.fori_loop(0, 36, body, 0)


B = 48


def x_stage(g, chip, core, yt, th, xf, xi, gt, ub, uo, f, u):
    unit = 2.0 * math.pi / N
    lane = lanes((8, 128))
    row = lax.broadcasted_iota(jnp.int32, (8, 128), 0)
    sign = jnp.where(lane < 64, 1.0, -1.0)
    kz = (3 * chip + g).astype(f32) * unit
    combos = [(t, c, s) for t in range(2) for c in range(3) for s in range(2)]
    at = lambda t, c, s: ((t * 3 + c) * 2 + s) * B
    tf = cat([xf[core, 0], xf[1 - core, 0], xf[core, 0], xf[1 - core, 0], xf[core, 1], xf[1 - core, 1]], 0)
    for ib in range(2):
        parts = []
        for t, c, s in combos:
            rows = pl.ds(96 * s + B * ib, B)
            zmc = 6 * g + 3 * t + c
            parts.append(cat([yt[core, zmc, rows, :], th[zmc, rows, :]], 1))
        hi, lo = split(cat(parts, 0))
        f[ib] = dot(cat([hi, lo, hi], 1), tf)
    for ib in range(2):
        for rt in range(B // 8):
            i0 = B * ib + 8 * rt
            ky = (2 * i0 + core + 2 * row).astype(f32) * unit
            for tl in range(3):
                kxs = (64 * tl + lane % 64).astype(f32) * unit * sign
                ls = pl.ds(128 * tl, 128)
                green = gt[pl.ds(pl.multiple_of(96 * g + i0, 8), 8), ls]
                pt = {k: f[ib, pl.ds(at(*k) + 8 * rt, 8), ls] * green for k in combos}
                for t in range(2):
                    dz = lambda c, s: (kz if t == 0 else -kz) * pt[1 - t, c, s]
                    for s in range(2):
                        dy = lambda c: (ky if s == 0 else -ky) * pt[t, c, 1 - s]
                        dx = lambda c: kxs * pltpu.roll(pt[t, c, s], 64, 1)
                        u[ib, pl.ds(at(t, 0, s) + 8 * rt, 8), ls] = dy(2) - dz(1, s)
                        u[ib, pl.ds(at(t, 1, s) + 8 * rt, 8), ls] = dz(0, s) - dx(2)
                        u[ib, pl.ds(at(t, 2, s) + 8 * rt, 8), ls] = dx(1) - dy(0)
    k0 = cat([xi[core, 0], xi[1 - core, 0]], 1)
    k1 = cat([xi[core, 1], xi[1 - core, 1]], 1)
    ti = cat([k0, k0, k1], 0)
    for ib in range(2):
        hi, lo = split(u[ib])
        back = dot(cat([hi, lo, hi], 1), ti)
        for t, c, s in combos:
            rows = pl.ds(96 * s + B * ib, B)
            zmc = 6 * g + 3 * t + c
            r0 = at(t, c, s)
            ub[core, zmc, rows, :] = back[r0 : r0 + B, :128]
            uo[zmc, rows, :] = back[r0 : r0 + B, 128:]


def y_backward(zm, ub, ty, out, o):
    lane = lanes((8, 128))
    rhs = cat([cat([ub[h, 3 * zm + c] for c in range(3)], 1) for h in range(2)], 0)
    hi, lo = split(rhs)
    o[...] = dot(ty[...], cat([hi, lo, hi], 0))
    for pp in range(4):
        for qh in range(2):
            for j in range(7):
                v = None
                for g in range((128 * j) // 24, min((128 * j + 127) // 24, 35) + 1):
                    y, c = divmod(g, 3)
                    t = o[pl.ds(8 * (2 * y + qh), 8), pl.ds(128 * c, 128)]
                    t = pltpu.roll(t, (24 * g - 128 * j - 24 * pp) % 128, 1)
                    v = t if v is None else jnp.where(lane >= 24 * g - 128 * j, t, v)
                out[zm, pp, qh, j] = v


def z_backward(g, v, zi, acc, flow):
    table = cat([zi[g, 0], zi[g, 0], zi[g, 1]], 1)
    for j in (0, 2, 4, 6):
        n = min(2, 7 - j)
        rhs = cat([v[:, 2 * g : 2 * g + 2, j + i].reshape(128, 128) for i in range(n)], 1)
        hi, lo = split(rhs)
        part = dot(table, cat([hi, lo, hi], 0))
        ls = pl.ds(128 * j, 128 * n)
        if g == 0:
            acc[:, ls] = part
        elif g == 1:
            acc[:, ls] = acc[:, ls] + part
        else:
            flow[ls, :] = (acc[:, ls] + part).T


def far_first(i):
    return (2 + i + i // 2 + 2 * (i // 3)) % 4


def flow_kernel(
    vort, zf_h, yf_h, xf_h, xi_h, yi_h, zi_h,
    flow, xr, yr,
    zf, yf, xf, xi, yi, zi, w, zt, rv, yt, th, ub, uo, bk, vv, gt, s, o, f, u, acc, xs,
    tsem, osem, fs, fr, bs, br, d1, d2, hs,
):
    p, q = lax.axis_index("px"), lax.axis_index("py")
    core, half, qc = q % 2, p // 4, q // 2
    other = q + 1 - 2 * core
    mz, my, mx = p % 4, 2 * half + q // 8, qc % 4
    chip = p * 8 + qc
    own = half == core
    loads = [
        pltpu.make_async_copy(a, b, tsem.at[i])
        for i, (a, b) in enumerate([(zf_h, zf), (yf_h, yf), (xf_h, xf), (xi_h, xi), (yi_h, yi), (zi_h, zi)])
    ]
    for cp in loads:
        cp.start()

    near = [(p > 0, (p - 1, q)), (p < 7, (p + 1, q)), (q > 0, (p, q - 1)), (q < 15, (p, q + 1))]
    bar = pltpu.get_barrier_semaphore()

    def greet(i, _):
        pl.semaphore_signal(bar, inc=1, device_id=(core * 4 + i // 16, i % 16), device_id_type=MESH)
        return 0

    lax.fori_loop(0, 64, greet, 0)
    pl.semaphore_signal(bar, inc=1, device_id=(p, other), device_id_type=MESH)
    for has, dev in near:
        @pl.when(has)
        def _(dev=dev):
            pl.semaphore_signal(bar, inc=1, device_id=dev, device_id_type=MESH)

    loads[0].wait()
    z_forward(vort, zf, zt.reshape(8, 6, 7, 8, 128), w)
    pl.semaphore_wait(bar, 65 + sum(has.astype(jnp.int32) for has, _ in near))

    def forward(i, _):
        g, n = i // 64, i % 64
        x, y, z = (mx + far_first(n // 16)) % 4, (my + far_first((n // 4) % 4)) % 4, (mz + far_first(n % 4)) % 4
        a, b = (y // 2) * 4 + z, (y % 2) * 4 + x
        sr = zt.at[a, pl.ds(2 * g, 2), :, b]
        ds = rv.at[pl.ds(2 * g, 2), p % 4, q // 8, :, q % 8]
        me = jnp.logical_and(n == 63, own)

        @pl.when(me)
        def _():
            pltpu.make_async_copy(sr, ds, fr.at[g]).start()

        @pl.when(jnp.logical_not(me))
        def _():
            pltpu.make_async_remote_copy(sr, ds, fs, fr.at[g], device_id=(a, 2 * b + half), device_id_type=MESH).start()

        return 0

    lax.fori_loop(0, 192, forward, 0)
    green_table(chip, core, gt)

    rows_in = rv.reshape(6, 4, 2, 7, 8, 128)
    rows_out = bk.reshape(6, 4, 2, 7, 8, 128)

    def swap1(g):
        return pltpu.make_async_remote_copy(
            yt.at[1 - core, pl.ds(6 * g, 6)], th.at[pl.ds(6 * g, 6)], d1.at[0, g], d1.at[1, g],
            device_id=(p, other), device_id_type=MESH,
        )

    def swap2(g):
        return pltpu.make_async_remote_copy(
            uo.at[pl.ds(6 * g, 6)], ub.at[core, pl.ds(6 * g, 6)], d2.at[0, g], d2.at[1, g],
            device_id=(p, other), device_id_type=MESH,
        )

    def arrive(g):
        t = rv.at[pl.ds(2 * g, 2)]
        pltpu.make_async_copy(t, t, fr.at[g]).wait()

        def one(t, _):
            y_forward(2 * g + t, rows_in, yf, yt, s)
            return 0

        lax.fori_loop(0, 2, one, 0)
        swap1(g).start()

    for cp in loads[1:]:
        cp.wait()
    arrive(0)

    def group(g, _):
        swap1(g).wait_recv()
        x_stage(g, chip, core, yt, th, xf, xi, gt, ub, uo, f, u)
        swap2(g).start()

        @pl.when(g < 2)
        def _():
            arrive(g + 1)

        swap2(g).wait_recv()

        def one(t, _):
            y_backward(2 * g + t, ub, yi, rows_out, o)
            return 0

        lax.fori_loop(0, 2, one, 0)

        def backward(n, _):
            x, z = (mx + far_first(n // 16)) % 4, (mz + far_first((n // 4) % 4)) % 4
            yl, cr = (q // 8 + 1 + (n // 2) % 2) % 2, (core + 1 + n % 2) % 2
            a, b = core * 4 + z, yl * 8 + 2 * x + cr
            sr = bk.at[pl.ds(2 * g, 2), z, b // 8, :, b % 8]
            ds = vv.at[p, pl.ds(2 * g, 2), :, qc]
            me = jnp.logical_and(n == 63, own)

            @pl.when(me)
            def _():
                pltpu.make_async_copy(sr, ds, br.at[g]).start()

            @pl.when(jnp.logical_not(me))
            def _():
                pltpu.make_async_remote_copy(sr, ds, bs, br.at[g], device_id=(a, b), device_id_type=MESH).start()

            return 0

        lax.fori_loop(0, 64, backward, 0)
        return 0

    lax.fori_loop(0, 3, group, 0)

    vin = vv.reshape(8, 6, 7, 8, 128)
    for g in range(3):
        t = vv.at[:, pl.ds(2 * g, 2)]
        pltpu.make_async_copy(t, t, br.at[g]).wait()
        z_backward(g, vin, zi, acc, flow)

    for m in range(9):
        for e, r0 in ((0, 0), (1, 22)):
            for i in range(4):
                xs[e, m, pl.ds(2 * i, 2), :] = flow[pl.ds(24 * (4 * m + i) + r0, 2), :]
    srcs = [xs.at[0], xs.at[1], flow.at[pl.ds(0, 144)], flow.at[pl.ds(720, 144)]]
    dsts = [xr.at[1], xr.at[0], yr.at[1], yr.at[0]]
    back = [1, 0, 3, 2]
    cps = []
    for k, (has, dev) in enumerate(near):
        cps.append(pltpu.make_async_remote_copy(srcs[k], dsts[k], hs.at[0, k], hs.at[1, k], device_id=dev, device_id_type=MESH))

        @pl.when(has)
        def _(k=k):
            cps[k].start()

    ends = [xr.at[0], xr.at[1], yr.at[0], yr.at[1]]
    for k, ref in enumerate(ends):
        @pl.when(jnp.logical_not(near[k][0]))
        def _(ref=ref):
            ref[...] = jnp.zeros(ref.shape, f32)

    for g in range(3):
        swap1(g).wait_send()
        swap2(g).wait_send()
    flat = [zt.reshape(2688, 1, 128), bk.reshape(2688, 1, 128)]
    for n, cond in ((63, own), (64, jnp.logical_not(own))):
        @pl.when(cond)
        def _(n=n):
            for ref, sem in zip(flat, (fs, bs)):
                t = ref.at[pl.ds(0, 42 * n)]
                pltpu.make_async_copy(t, t, sem).wait()

    for k, (has, dev) in enumerate(near):
        @pl.when(has)
        def _(k=k):
            cps[k].wait_send()
            cps[back[k]].wait_recv()


def stretch_kernel(vort, flow, xr, yr, vel, st, pad):
    for i in range(36):
        pad[i, pl.ds(8, 24), :] = flow[pl.ds(24 * i, 24), :]
        pad[i, pl.ds(6, 2), :] = xr[0, i // 4, pl.ds(2 * (i % 4), 2), :]
        pad[i, pl.ds(32, 2), :] = xr[1, i // 4, pl.ds(2 * (i % 4), 2), :]

    def at_y(y, c):
        if y < 0:
            return yr[0, pl.ds(((y + 2) * 3 + c) * 24, 24), :]
        if y >= 12:
            return yr[1, pl.ds(((y - 12) * 3 + c) * 24, 24), :]
        return flow[pl.ds(24 * (3 * y + c), 24), :]

    def diff(m2, m1, p1, p2):
        return (8.0 * (p1 - m1) - (p2 - m2)) * (1.0 / 12.0)

    lane = lanes((24, 128))

    def put(out, c, yp, t):
        (a0, b0), (a1, b1) = [(v[:, :128], v[:, 128:]) for v in t]
        ra, rb = pltpu.roll(a1, 64, 1), pltpu.roll(b1, 64, 1)
        out[c, :, pl.ds(384 * yp, 128)] = a0
        out[c, :, pl.ds(384 * yp + 128, 128)] = jnp.where(lane < 64, b0, ra)
        out[c, :, pl.ds(384 * yp + 256, 128)] = jnp.where(lane < 64, ra, rb)

    for yp in range(6):
        fields = [[cat(padded_line(vort, d, 2 * yp + e, lane), 1) for d in range(3)] for e in range(2)]
        for c in range(3):
            t, vs = [], []
            for e in range(2):
                y = 2 * yp + e
                i = 3 * y + c
                wv = fields[e]
                dx = diff(*[pad[i, pl.ds(8 + k, 24), :] for k in (-2, -1, 1, 2)])
                dy = diff(*[at_y(y + k, c) for k in (-2, -1, 1, 2)])
                cur = at_y(y, c)
                dz = diff(*[pltpu.roll(cur, (-k) % 256, 1) for k in (-2, -1, 1, 2)])
                t.append(wv[0] * dx + wv[1] * dy + wv[2] * dz)
                vs.append(cur)
            put(vel, c, yp, vs)
            put(st, c, yp, t)


def sds(*shape):
    return jax.ShapeDtypeStruct(shape, f32)


def on_device(tb, vort):
    vspec, aspec = pl.BlockSpec(memory_space=VMEM), pl.BlockSpec(memory_space=ANY)
    dma = pltpu.SemaphoreType.DMA
    flow, xr, yr = pl.pallas_call(
        flow_kernel,
        out_shape=[sds(896, 256), sds(2, 9, 8, 256), sds(2, 144, 256)],
        in_specs=[vspec] + [aspec] * 6,
        out_specs=[vspec] * 3,
        scratch_shapes=[VMEM(t.shape, bf16) for t in tb]
        + [
            VMEM((896, 256), f32), VMEM((8, 6, 7, 8, 1, 128), f32), VMEM((6, 4, 2, 7, 8, 1, 128), f32),
            VMEM((2, 18, 192, 128), f32), VMEM((18, 192, 128), f32), VMEM((2, 18, 192, 128), f32),
            VMEM((18, 192, 128), f32), VMEM((6, 4, 2, 7, 8, 1, 128), f32), VMEM((8, 6, 7, 8, 1, 128), f32),
            VMEM((288, 384), f32), VMEM((192, 384), f32), VMEM((192, 384), f32),
            VMEM((2, 576, 384), f32), VMEM((2, 576, 384), f32), VMEM((256, 896), f32), VMEM((2, 9, 8, 256), f32),
            dma((6,)), dma((2,)), dma, dma((3,)), dma, dma((3,)), dma((2, 3)), dma((2, 3)), dma((2, 4)),
        ],
        compiler_params=pltpu.CompilerParams(collective_id=0, has_side_effects=True, vmem_limit_bytes=62 * 1024 * 1024),
    )(vort, *tb)
    return pl.pallas_call(
        stretch_kernel,
        out_shape=[sds(3, 24, 2304), sds(3, 24, 2304)],
        in_specs=[vspec] * 4,
        out_specs=[vspec] * 2,
        scratch_shapes=[VMEM((36, 40, 256), f32)],
        compiler_params=pltpu.CompilerParams(vmem_limit_bytes=40 * 1024 * 1024),
    )(vort, flow, xr, yr)


def solution(mesh):
    tb = [jnp.asarray(v) for v in tables()]
    return jax.shard_map(
        functools.partial(on_device, tb), mesh=mesh, in_specs=(P(None, "px", "py"),),
        out_specs=(P(None, "px", "py"), P(None, "px", "py")), check_vma=False,
    )
```

profile of v0, /device:TPU:1, one launch (start us, length us, event | category | flops | bytes accessed | tf_op | source)
XLA Modules:
  0.0 78.9 jit_solution(5085613360371402315)
XLA Ops:
  0.6 0.0 copy-start
  0.6 71.6 %shard_map.86 = (f32[896,256]{1,0:T(8,128)}, f32[2,9,8,256]{3,2,1,0:T(8,128)}, f32[2,144,256]{2,1,0:T(8,128)}) custom-call(f32[3,24,2304]{2,1,0:T(8,128)} %vort.3, bf16[2,384,256]{2,1,0:T(8,128)(2,1)} %constant.12.clone.zf_h, bf16[384,576]{1,0:T(8,128)(2,1)} %constant.13.clone.yf_h, bf16[2,2,128,384]{3,2,1,0:T(8,128)(2,1)} %constant.14.clone.xf_h, ...), custom_call_target="tpu_custom_call" | custom-call | tf_op jit(solution)/shard_map/pallas_call | solution.py:452
  72.3 0.0 copy-done
  72.3 0.0 copy-start.1
  72.3 1.2 %copy-done.1 = f32[896,256]{1,0:T(8,128)S(1)} copy-done((f32[896,256]{1,0:T(8,128)S(1)}, f32[896,256]{1,0:T(8,128)}, u32[]{:S(2)}) %copy-start.1) | copy-done | bytes 917528
  73.5 0.0 copy-start.2
  73.5 1.0 %copy-done.2 = f32[2,144,256]{2,1,0:T(8,128)S(1)} copy-done((f32[2,144,256]{2,1,0:T(8,128)S(1)}, f32[2,144,256]{2,1,0:T(8,128)}, u32[]{:S(2)}) %copy-start.2) | copy-done | bytes 294936
  74.4 0.0 copy-start.3
  74.4 0.9 %copy-done.3 = f32[2,9,8,256]{3,2,1,0:T(8,128)S(1)} copy-done((f32[2,9,8,256]{3,2,1,0:T(8,128)S(1)}, f32[2,9,8,256]{3,2,1,0:T(8,128)}, u32[]{:S(2)}) %copy-start.3) | copy-done | bytes 147480
  75.3 3.5 %shard_map.87 = (f32[3,24,2304]{2,1,0:T(8,128)}, f32[3,24,2304]{2,1,0:T(8,128)}) custom-call(f32[3,24,2304]{2,1,0:T(8,128)S(1)} %copy-done, f32[896,256]{1,0:T(8,128)S(1)} %copy-done.1, f32[2,9,8,256]{3,2,1,0:T(8,128)S(1)} %copy-done.3, f32[2,144,256]{2,1,0:T(8,128)S(1)} %copy-done.2), custom_call_target="tpu_custom_call" | custom-call | tf_op jit(solution)/shard_map/pallas_call | solution.py:468
Async XLA Ops:
  0.6 71.6 %copy-start = (f32[3,24,2304]{2,1,0:T(8,128)S(1)}, f32[3,24,2304]{2,1,0:T(8,128)}, u32[]{:S(2)}) copy-start(f32[3,24,2304]{2,1,0:T(8,128)} %vort.3) | copy-start | bytes 1990660
  72.3 1.2 %copy-start.1 = (f32[896,256]{1,0:T(8,128)S(1)}, f32[896,256]{1,0:T(8,128)}, u32[]{:S(2)}) copy-start(f32[896,256]{1,0:T(8,128)} %get-tuple-element.5.flow) | copy-start | bytes 2752516
  73.5 1.0 %copy-start.2 = (f32[2,144,256]{2,1,0:T(8,128)S(1)}, f32[2,144,256]{2,1,0:T(8,128)}, u32[]{:S(2)}) copy-start(f32[2,144,256]{2,1,0:T(8,128)} %get-tuple-element.7.yr) | copy-start | bytes 884740
  74.4 0.9 %copy-start.3 = (f32[2,9,8,256]{3,2,1,0:T(8,128)S(1)}, f32[2,9,8,256]{3,2,1,0:T(8,128)}, u32[]{:S(2)}) copy-start(f32[2,9,8,256]{3,2,1,0:T(8,128)} %get-tuple-element.6.xr) | copy-start | bytes 442372
where the time goes:
time: 79.4 us; the launch traced here: 78.9 us
  Pallas kernels  75.1 us (95%)
  local copies, waits for them, and re-layouts  3.05 us (4%)
    pallas_call x1, Pallas kernels, on_device(): pl.pallas_call(flow_kernel, out_shape=[sds(896, 256), sds(2, 9, 8, 256),...  71.6 us
    pallas_call x1, Pallas kernels, on_device(): pl.pallas_call(stretch_kernel, out_shape=[sds(3, 24, 2304), sds(3, 24, 23...  3.52 us
    unnamed x8, local copies, waits for them, and re-layouts  3.05 us

commit v1 on v0

--- a/solution.py
+++ b/solution.py
@@ -1,5 +1,6 @@
 import math
 import functools
+import itertools
 
 import numpy as np
 import jax
@@ -47,7 +48,7 @@
     yi = (yf * weight(my)[:, None]).T
     mx, tx = 64 * (r // 128) + r % 64, (r // 64) % 2
     lane = np.arange(128)
-    jx = 96 * np.arange(2)[:, None] + lane[None]
+    jx = 24 * (2 * (lane[None] // 24) + np.arange(2)[:, None]) + lane[None] % 24
     xf = np.where(lane[None, :, None] < 96, trig(mx[None, None], tx[None, None], jx[:, :, None]), 0.0)
     xi = np.swapaxes(xf * weight(mx)[None, None], 1, 2)
     stack = lambda t: np.stack(pair_np(t), axis=-3)
@@ -98,7 +99,8 @@
             out[:, :, blk // 128 + jj] = acc[:, 128 * jj : 128 * jj + 128].reshape(8, 6, 8, 128)
 
 
-def y_forward(zm, r, ty, out, s):
+def y_forward(g, h2, r, ty, out, s):
+    zm = 2 * g + h2
     lane = lanes((8, 128))
     zero = jnp.zeros((8, 128), f32)
     for y in range(12):
@@ -107,9 +109,9 @@
             for qh in range(2):
                 v = zero
                 for pp in (3, 2, 1, 0):
-                    t = r[zm, pp, qh, j]
+                    t = r[g, pp, qh, h2, j]
                     if o + 24 > 128:
-                        t = jnp.where(lane >= o, t, r[zm, pp, qh, j + 1])
+                        t = jnp.where(lane >= o, t, r[g, pp, qh, h2, j + 1])
                     t = pltpu.roll(t, (24 * pp - o) % 128, 1)
                     v = jnp.where(lane < 24 * pp + 24, t, v)
                 s[pl.ds(8 * (2 * y + qh), 8), pl.ds(128 * c, 128)] = v
@@ -189,7 +191,8 @@
             uo[zmc, rows, :] = back[r0 : r0 + B, 128:]
 
 
-def y_backward(zm, ub, ty, out, o):
+def y_backward(g, h2, ub, ty, out, o):
+    zm = 2 * g + h2
     lane = lanes((8, 128))
     rhs = cat([cat([ub[h, 3 * zm + c] for c in range(3)], 1) for h in range(2)], 0)
     hi, lo = split(rhs)
@@ -198,12 +201,12 @@
         for qh in range(2):
             for j in range(7):
                 v = None
-                for g in range((128 * j) // 24, min((128 * j + 127) // 24, 35) + 1):
-                    y, c = divmod(g, 3)
+                for i in range((128 * j) // 24, min((128 * j + 127) // 24, 35) + 1):
+                    y, c = divmod(i, 3)
                     t = o[pl.ds(8 * (2 * y + qh), 8), pl.ds(128 * c, 128)]
-                    t = pltpu.roll(t, (24 * g - 128 * j - 24 * pp) % 128, 1)
-                    v = t if v is None else jnp.where(lane >= 24 * g - 128 * j, t, v)
-                out[zm, pp, qh, j] = v
+                    t = pltpu.roll(t, (24 * i - 128 * j - 24 * pp) % 128, 1)
+                    v = t if v is None else jnp.where(lane >= 24 * i - 128 * j, t, v)
+                out[g, pp, qh, h2, j] = v
 
 
 def z_backward(g, v, zi, acc, flow):
@@ -222,25 +225,29 @@
             flow[ls, :] = (acc[:, ls] + part).T
 
 
-def far_first(i):
-    return (2 + i + i // 2 + 2 * (i // 3)) % 4
+def hops(offset):
+    return sum(min(v, 4 - v) for v in offset)
+
+
+OFFSETS = sorted(itertools.product((2, 1, 3, 0), repeat=3), key=hops, reverse=True)
+HALF = [d for d in OFFSETS if d[2] % 2 == 0]
 
 
 def flow_kernel(
-    vort, zf_h, yf_h, xf_h, xi_h, yi_h, zi_h,
+    vort_h, zf_h, yf_h, xf_h, xi_h, yi_h, zi_h,
     flow, xr, yr,
-    zf, yf, xf, xi, yi, zi, w, zt, rv, yt, th, ub, uo, bk, vv, gt, s, o, f, u, acc, xs,
-    tsem, osem, fs, fr, bs, br, d1, d2, hs,
+    zf, yf, xf, xi, yi, zi, vort, w, zt, rv, yt, th, ub, uo, bk, vv, gt, s, o, f, u, acc, xs,
+    tsem, fs, fr, bs, br, d1, d2, hs,
 ):
     p, q = lax.axis_index("px"), lax.axis_index("py")
-    core, half, qc = q % 2, p // 4, q // 2
+    core, half, qc = q % 2, p % 2, q // 2
     other = q + 1 - 2 * core
-    mz, my, mx = p % 4, 2 * half + q // 8, qc % 4
+    mz, my, mx = p % 4, 2 * (p // 4) + q // 8, qc % 4
     chip = p * 8 + qc
     own = half == core
     loads = [
         pltpu.make_async_copy(a, b, tsem.at[i])
-        for i, (a, b) in enumerate([(zf_h, zf), (yf_h, yf), (xf_h, xf), (xi_h, xi), (yi_h, yi), (zi_h, zi)])
+        for i, (a, b) in enumerate([(vort_h, vort), (zf_h, zf), (yf_h, yf), (xf_h, xf), (xi_h, xi), (yi_h, yi), (zi_h, zi)])
     ]
     for cp in loads:
         cp.start()
@@ -248,11 +255,8 @@
     near = [(p > 0, (p - 1, q)), (p < 7, (p + 1, q)), (q > 0, (p, q - 1)), (q < 15, (p, q + 1))]
     bar = pltpu.get_barrier_semaphore()
 
-    def greet(i, _):
-        pl.semaphore_signal(bar, inc=1, device_id=(core * 4 + i // 16, i % 16), device_id_type=MESH)
-        return 0
-
-    lax.fori_loop(0, 64, greet, 0)
+    for i in range(64):
+        pl.semaphore_signal(bar, inc=1, device_id=(2 * (i // 16) + core, i % 16), device_id_type=MESH)
     pl.semaphore_signal(bar, inc=1, device_id=(p, other), device_id_type=MESH)
     for has, dev in near:
         @pl.when(has)
@@ -260,36 +264,43 @@
             pl.semaphore_signal(bar, inc=1, device_id=dev, device_id_type=MESH)
 
     loads[0].wait()
+    loads[1].wait()
     z_forward(vort, zf, zt.reshape(8, 6, 7, 8, 128), w)
     pl.semaphore_wait(bar, 65 + sum(has.astype(jnp.int32) for has, _ in near))
 
-    def forward(i, _):
-        g, n = i // 64, i % 64
-        x, y, z = (mx + far_first(n // 16)) % 4, (my + far_first((n // 4) % 4)) % 4, (mz + far_first(n % 4)) % 4
-        a, b = (y // 2) * 4 + z, (y % 2) * 4 + x
-        sr = zt.at[a, pl.ds(2 * g, 2), :, b]
-        ds = rv.at[pl.ds(2 * g, 2), p % 4, q // 8, :, q % 8]
-        me = jnp.logical_and(n == 63, own)
-
-        @pl.when(me)
+    def send(cond, sr, ds, ssem, rsem, dev):
+        remote = pltpu.make_async_remote_copy(sr, ds, ssem, rsem, device_id=dev, device_id_type=MESH)
+        if cond is None:
+            remote.start()
+            return
+
+        @pl.when(cond)
         def _():
-            pltpu.make_async_copy(sr, ds, fr.at[g]).start()
-
-        @pl.when(jnp.logical_not(me))
+            pltpu.make_async_copy(sr, ds, rsem).start()
+
+        @pl.when(jnp.logical_not(cond))
         def _():
-            pltpu.make_async_remote_copy(sr, ds, fs, fr.at[g], device_id=(a, 2 * b + half), device_id_type=MESH).start()
-
+            remote.start()
+
+    def forward(g, _):
+        ds = rv.at[g, p // 2, q // 8, :, :, q % 8]
+        for dx, dy, dz in OFFSETS:
+            x, y, z = (mx + dx) % 4, (my + dy) % 4, (mz + dz) % 4
+            a, b = (y // 2) * 4 + z, (y % 2) * 4 + x
+            last = own if (dx, dy, dz) == (0, 0, 0) else None
+            send(last, zt.at[a, pl.ds(2 * g, 2), :, b], ds, fs, fr.at[g], (a, 2 * b + half))
         return 0
 
-    lax.fori_loop(0, 192, forward, 0)
+    lax.fori_loop(0, 3, forward, 0)
     green_table(chip, core, gt)
 
-    rows_in = rv.reshape(6, 4, 2, 7, 8, 128)
-    rows_out = bk.reshape(6, 4, 2, 7, 8, 128)
-
-    def swap1(g):
+    rows_in = rv.reshape(3, 4, 2, 2, 7, 8, 128)
+    rows_out = bk.reshape(3, 4, 2, 2, 7, 8, 128)
+
+    def swap1(g, t):
+        rows = pl.ds(6 * g + 3 * t, 3)
         return pltpu.make_async_remote_copy(
-            yt.at[1 - core, pl.ds(6 * g, 6)], th.at[pl.ds(6 * g, 6)], d1.at[0, g], d1.at[1, g],
+            yt.at[1 - core, rows], th.at[rows], d1.at[0, g, t], d1.at[1, g, t],
             device_id=(p, other), device_id_type=MESH,
         )
 
@@ -300,22 +311,23 @@
         )
 
     def arrive(g):
-        t = rv.at[pl.ds(2 * g, 2)]
+        t = rv.at[g]
         pltpu.make_async_copy(t, t, fr.at[g]).wait()
 
         def one(t, _):
-            y_forward(2 * g + t, rows_in, yf, yt, s)
+            y_forward(g, t, rows_in, yf, yt, s)
+            swap1(g, t).start()
             return 0
 
         lax.fori_loop(0, 2, one, 0)
-        swap1(g).start()
-
-    for cp in loads[1:]:
+
+    for cp in loads[2:]:
         cp.wait()
     arrive(0)
 
     def group(g, _):
-        swap1(g).wait_recv()
+        swap1(g, 0).wait_recv()
+        swap1(g, 1).wait_recv()
         x_stage(g, chip, core, yt, th, xf, xi, gt, ub, uo, f, u)
         swap2(g).start()
 
@@ -326,30 +338,18 @@
         swap2(g).wait_recv()
 
         def one(t, _):
-            y_backward(2 * g + t, ub, yi, rows_out, o)
+            y_backward(g, t, ub, yi, rows_out, o)
             return 0
 
         lax.fori_loop(0, 2, one, 0)
 
-        def backward(n, _):
-            x, z = (mx + far_first(n // 16)) % 4, (mz + far_first((n // 4) % 4)) % 4
-            yl, cr = (q // 8 + 1 + (n // 2) % 2) % 2, (core + 1 + n % 2) % 2
-            a, b = core * 4 + z, yl * 8 + 2 * x + cr
-            sr = bk.at[pl.ds(2 * g, 2), z, b // 8, :, b % 8]
-            ds = vv.at[p, pl.ds(2 * g, 2), :, qc]
-            me = jnp.logical_and(n == 63, own)
-
-            @pl.when(me)
-            def _():
-                pltpu.make_async_copy(sr, ds, br.at[g]).start()
-
-            @pl.when(jnp.logical_not(me))
-            def _():
-                pltpu.make_async_remote_copy(sr, ds, bs, br.at[g], device_id=(a, b), device_id_type=MESH).start()
-
-            return 0
-
-        lax.fori_loop(0, 64, backward, 0)
+        ds = vv.at[p, pl.ds(2 * g, 2), :, qc]
+        for dx, dy, dz in HALF:
+            x, y, z = (mx + dx) % 4, (my + dy) % 4, (mz + dz + (half + core) % 2) % 4
+            for dc in (1, 0):
+                a, b = (y // 2) * 4 + z, (y % 2) * 8 + 2 * x + (core + dc) % 2
+                last = own if (dx, dy, dz, dc) == (0, 0, 0, 0) else None
+                send(last, bk.at[g, a // 2, b // 8, :, :, b % 8], ds, bs, br.at[g], (a, b))
         return 0
 
     lax.fori_loop(0, 3, group, 0)
@@ -382,7 +382,8 @@
             ref[...] = jnp.zeros(ref.shape, f32)
 
     for g in range(3):
-        swap1(g).wait_send()
+        swap1(g, 0).wait_send()
+        swap1(g, 1).wait_send()
         swap2(g).wait_send()
     flat = [zt.reshape(2688, 1, 128), bk.reshape(2688, 1, 128)]
     for n, cond in ((63, own), (64, jnp.logical_not(own))):
@@ -452,18 +453,18 @@
     flow, xr, yr = pl.pallas_call(
         flow_kernel,
         out_shape=[sds(896, 256), sds(2, 9, 8, 256), sds(2, 144, 256)],
-        in_specs=[vspec] + [aspec] * 6,
+        in_specs=[aspec] * 7,
         out_specs=[vspec] * 3,
         scratch_shapes=[VMEM(t.shape, bf16) for t in tb]
         + [
-            VMEM((896, 256), f32), VMEM((8, 6, 7, 8, 1, 128), f32), VMEM((6, 4, 2, 7, 8, 1, 128), f32),
+            VMEM((3, 24, 2304), f32), VMEM((896, 256), f32), VMEM((8, 6, 7, 8, 1, 128), f32), VMEM((3, 4, 2, 2, 7, 8, 1, 128), f32),
             VMEM((2, 18, 192, 128), f32), VMEM((18, 192, 128), f32), VMEM((2, 18, 192, 128), f32),
-            VMEM((18, 192, 128), f32), VMEM((6, 4, 2, 7, 8, 1, 128), f32), VMEM((8, 6, 7, 8, 1, 128), f32),
+            VMEM((18, 192, 128), f32), VMEM((3, 4, 2, 2, 7, 8, 1, 128), f32), VMEM((8, 6, 7, 8, 1, 128), f32),
             VMEM((288, 384), f32), VMEM((192, 384), f32), VMEM((192, 384), f32),
             VMEM((2, 576, 384), f32), VMEM((2, 576, 384), f32), VMEM((256, 896), f32), VMEM((2, 9, 8, 256), f32),
-            dma((6,)), dma((2,)), dma, dma((3,)), dma, dma((3,)), dma((2, 3)), dma((2, 3)), dma((2, 4)),
+            dma((7,)), dma, dma((3,)), dma, dma((3,)), dma((2, 3, 2)), dma((2, 3)), dma((2, 4)),
         ],
-        compiler_params=pltpu.CompilerParams(collective_id=0, has_side_effects=True, vmem_limit_bytes=62 * 1024 * 1024),
+        compiler_params=pltpu.CompilerParams(collective_id=0, has_side_effects=True, vmem_limit_bytes=60 * 1024 * 1024),
     )(vort, *tb)
     return pl.pallas_call(
         stretch_kernel,
@@ -471,7 +472,7 @@
         in_specs=[vspec] * 4,
         out_specs=[vspec] * 2,
         scratch_shapes=[VMEM((36, 40, 256), f32)],
-        compiler_params=pltpu.CompilerParams(vmem_limit_bytes=40 * 1024 * 1024),
+        compiler_params=pltpu.CompilerParams(vmem_limit_bytes=61 * 1024 * 1024),
     )(vort, flow, xr, yr)
 
 

time: 79.4 us -> 60.4 us (0.76)
  Pallas kernels: 75.1 us -> 59.6 us
  local copies, waits for them, and re-layouts: 3.05 us -> 0 us
    pallas_call x1, Pallas kernels: 71.6 us -> 54.6 us  [on_device(): pl.pallas_call(flow_kernel, out_shape=[sds(896, 256), sds(2, 9, 8, 256),...]
    unnamed x8 -> x0, local copies, waits for them, and re-layouts: 3.05 us -> none
    pallas_call x1, Pallas kernels: 3.52 us -> 5.02 us  [on_device(): pl.pallas_call(stretch_kernel, out_shape=[sds(3, 24, 2304), sds(3, 24, 23...]
where the time goes in v1:
time: 60.4 us; the launch traced here: 60.3 us
  Pallas kernels  59.6 us (99%)
  between operations  0.64 us (1%)
    pallas_call x1, Pallas kernels, on_device(): pl.pallas_call(flow_kernel, out_shape=[sds(896, 256), sds(2, 9, 8, 256),...  54.6 us
    pallas_call x1, Pallas kernels, on_device(): pl.pallas_call(stretch_kernel, out_shape=[sds(3, 24, 2304), sds(3, 24, 23...  5.02 us

profile of v1, /device:TPU:1, one launch (start us, length us, event | category | flops | bytes accessed | tf_op | source)
XLA Modules:
  0.0 60.3 jit_solution(8426547322245295866)
XLA Ops:
  0.6 54.6 %shard_map.86 = (f32[896,256]{1,0:T(8,128)}, f32[2,9,8,256]{3,2,1,0:T(8,128)}, f32[2,144,256]{2,1,0:T(8,128)}) custom-call(f32[3,24,2304]{2,1,0:T(8,128)} %vort.1, bf16[2,384,256]{2,1,0:T(8,128)(2,1)} %constant.12.clone.zf_h, bf16[384,576]{1,0:T(8,128)(2,1)} %constant.13.clone.yf_h, bf16[2,2,128,384]{3,2,1,0:T(8,128)(2,1)} %constant.14.clone.xf_h, ...), custom_call_target="tpu_custom_call" | custom-call | tf_op jit(solution)/shard_map/pallas_call | solution.py:453
  55.3 5.0 %shard_map.87 = (f32[3,24,2304]{2,1,0:T(8,128)}, f32[3,24,2304]{2,1,0:T(8,128)}) custom-call(f32[3,24,2304]{2,1,0:T(8,128)} %vort.1, f32[896,256]{1,0:T(8,128)} %get-tuple-element.5.flow, f32[2,9,8,256]{3,2,1,0:T(8,128)} %get-tuple-element.6.xr, f32[2,144,256]{2,1,0:T(8,128)} %get-tuple-element.7.yr), custom_call_target="tpu_custom_call" | custom-call | tf_op jit(solution)/shard_map/pallas_call | solution.py:469

commit v2 on v1

--- a/solution.py
+++ b/solution.py
@@ -225,6 +225,64 @@
             flow[ls, :] = (acc[:, ls] + part).T
 
 
+def diff(m2, m1, p1, p2):
+    return (8.0 * (p1 - m1) - (p2 - m2)) * (1.0 / 12.0)
+
+
+def put(out, c, yp, pair):
+    lane = lanes((24, 128))
+    (a0, b0), (a1, b1) = [(v[:, :128], v[:, 128:]) for v in pair]
+    ra, rb = pltpu.roll(a1, 64, 1), pltpu.roll(b1, 64, 1)
+    out[c, :, pl.ds(384 * yp, 128)] = a0
+    out[c, :, pl.ds(384 * yp + 128, 128)] = jnp.where(lane < 64, b0, ra)
+    out[c, :, pl.ds(384 * yp + 256, 128)] = jnp.where(lane < 64, ra, rb)
+
+
+def inner_stretch(flow, w, part):
+    row = lax.broadcasted_iota(jnp.int32, (24, 256), 0)
+    zero = jnp.zeros((24, 256), f32)
+    for y in range(12):
+        for c in range(3):
+            i = 3 * y + c
+            line = lambda k: flow[pl.ds(24 * (3 * k + c), 24), :] if 0 <= k < 12 else zero
+            cur = line(y)
+            dx = diff(*[
+                jnp.where(jnp.logical_and(row + k >= 0, row + k < 24), pltpu.roll(cur, (-k) % 24, 0), zero)
+                for k in (-2, -1, 1, 2)
+            ])
+            dy = diff(*[line(y + k) for k in (-2, -1, 1, 2)])
+            dz = diff(*[pltpu.roll(cur, (-k) % 256, 1) for k in (-2, -1, 1, 2)])
+            wv = [w[pl.ds(72 * y + 24 * d, 24), :] for d in range(3)]
+            part[pl.ds(24 * i, 24), :] = wv[0] * dx + wv[1] * dy + wv[2] * dz
+
+
+def edge_stretch(w, part, xr, yr, top, low, st):
+    zero = jnp.zeros((24, 256), f32)
+    for i in range(36):
+        top[i, pl.ds(6, 2), :] = xr[0, i // 4, pl.ds(2 * (i % 4), 2), :]
+        low[i, pl.ds(10, 2), :] = xr[1, i // 4, pl.ds(2 * (i % 4), 2), :]
+    for yp in range(6):
+        for c in range(3):
+            pair = []
+            for y in (2 * yp, 2 * yp + 1):
+                i = 3 * y + c
+                v = part[pl.ds(24 * i, 24), :]
+                wx = w[pl.ds(72 * y, 24), :]
+                head = diff(*[top[i, pl.ds(8 + k, 8), :] for k in (-2, -1, 1, 2)])
+                tail = diff(*[low[i, pl.ds(2 + k, 8), :] for k in (-2, -1, 1, 2)])
+                v = cat([v[0:8] + wx[0:8] * head, v[8:16], v[16:24] + wx[16:24] * tail], 0)
+                if y < 2 or y > 9:
+                    def line(k):
+                        if k < 0:
+                            return yr[0, pl.ds(((k + 2) * 3 + c) * 24, 24), :]
+                        return yr[1, pl.ds(((k - 12) * 3 + c) * 24, 24), :] if k >= 12 else zero
+
+                    dy = diff(*[line(y + k) for k in (-2, -1, 1, 2)])
+                    v = v + w[pl.ds(72 * y + 24, 24), :] * dy
+                pair.append(v)
+            put(st, c, yp, pair)
+
+
 def hops(offset):
     return sum(min(v, 4 - v) for v in offset)
 
@@ -235,9 +293,10 @@
 
 def flow_kernel(
     vort_h, zf_h, yf_h, xf_h, xi_h, yi_h, zi_h,
-    flow, xr, yr,
+    vel_h, st_h,
     zf, yf, xf, xi, yi, zi, vort, w, zt, rv, yt, th, ub, uo, bk, vv, gt, s, o, f, u, acc, xs,
-    tsem, fs, fr, bs, br, d1, d2, hs,
+    flow, xr, yr, vel, st, part, top, low,
+    tsem, fs, fr, bs, br, d1, d2, hs, os,
 ):
     p, q = lax.axis_index("px"), lax.axis_index("py")
     core, half, qc = q % 2, p % 2, q // 2
@@ -293,6 +352,8 @@
 
     lax.fori_loop(0, 3, forward, 0)
     green_table(chip, core, gt)
+    top[...] = jnp.zeros(top.shape, f32)
+    low[...] = jnp.zeros(low.shape, f32)
 
     rows_in = rv.reshape(3, 4, 2, 2, 7, 8, 128)
     rows_out = bk.reshape(3, 4, 2, 2, 7, 8, 128)
@@ -344,9 +405,9 @@
         lax.fori_loop(0, 2, one, 0)
 
         ds = vv.at[p, pl.ds(2 * g, 2), :, qc]
-        for dx, dy, dz in HALF:
-            x, y, z = (mx + dx) % 4, (my + dy) % 4, (mz + dz + (half + core) % 2) % 4
-            for dc in (1, 0):
+        for dc in (1, 0):
+            for dx, dy, dz in HALF:
+                x, y, z = (mx + dx) % 4, (my + dy) % 4, (mz + dz + (half + core) % 2) % 4
                 a, b = (y // 2) * 4 + z, (y % 2) * 8 + 2 * x + (core + dc) % 2
                 last = own if (dx, dy, dz, dc) == (0, 0, 0, 0) else None
                 send(last, bk.at[g, a // 2, b // 8, :, :, b % 8], ds, bs, br.at[g], (a, b))
@@ -380,6 +441,13 @@
         @pl.when(jnp.logical_not(near[k][0]))
         def _(ref=ref):
             ref[...] = jnp.zeros(ref.shape, f32)
+
+    for yp in range(6):
+        for c in range(3):
+            put(vel, c, yp, [flow[pl.ds(24 * (3 * (2 * yp + e) + c), 24), :] for e in range(2)])
+    out_vel = pltpu.make_async_copy(vel, vel_h, os.at[0])
+    out_vel.start()
+    inner_stretch(flow, w, part)
 
     for g in range(3):
         swap1(g, 0).wait_send()
@@ -399,48 +467,11 @@
             cps[k].wait_send()
             cps[back[k]].wait_recv()
 
-
-def stretch_kernel(vort, flow, xr, yr, vel, st, pad):
-    for i in range(36):
-        pad[i, pl.ds(8, 24), :] = flow[pl.ds(24 * i, 24), :]
-        pad[i, pl.ds(6, 2), :] = xr[0, i // 4, pl.ds(2 * (i % 4), 2), :]
-        pad[i, pl.ds(32, 2), :] = xr[1, i // 4, pl.ds(2 * (i % 4), 2), :]
-
-    def at_y(y, c):
-        if y < 0:
-            return yr[0, pl.ds(((y + 2) * 3 + c) * 24, 24), :]
-        if y >= 12:
-            return yr[1, pl.ds(((y - 12) * 3 + c) * 24, 24), :]
-        return flow[pl.ds(24 * (3 * y + c), 24), :]
-
-    def diff(m2, m1, p1, p2):
-        return (8.0 * (p1 - m1) - (p2 - m2)) * (1.0 / 12.0)
-
-    lane = lanes((24, 128))
-
-    def put(out, c, yp, t):
-        (a0, b0), (a1, b1) = [(v[:, :128], v[:, 128:]) for v in t]
-        ra, rb = pltpu.roll(a1, 64, 1), pltpu.roll(b1, 64, 1)
-        out[c, :, pl.ds(384 * yp, 128)] = a0
-        out[c, :, pl.ds(384 * yp + 128, 128)] = jnp.where(lane < 64, b0, ra)
-        out[c, :, pl.ds(384 * yp + 256, 128)] = jnp.where(lane < 64, ra, rb)
-
-    for yp in range(6):
-        fields = [[cat(padded_line(vort, d, 2 * yp + e, lane), 1) for d in range(3)] for e in range(2)]
-        for c in range(3):
-            t, vs = [], []
-            for e in range(2):
-                y = 2 * yp + e
-                i = 3 * y + c
-                wv = fields[e]
-                dx = diff(*[pad[i, pl.ds(8 + k, 24), :] for k in (-2, -1, 1, 2)])
-                dy = diff(*[at_y(y + k, c) for k in (-2, -1, 1, 2)])
-                cur = at_y(y, c)
-                dz = diff(*[pltpu.roll(cur, (-k) % 256, 1) for k in (-2, -1, 1, 2)])
-                t.append(wv[0] * dx + wv[1] * dy + wv[2] * dz)
-                vs.append(cur)
-            put(vel, c, yp, vs)
-            put(st, c, yp, t)
+    edge_stretch(w, part, xr, yr, top, low, st)
+    out_st = pltpu.make_async_copy(st, st_h, os.at[1])
+    out_st.start()
+    out_vel.wait()
+    out_st.wait()
 
 
 def sds(*shape):
@@ -450,11 +481,11 @@
 def on_device(tb, vort):
     vspec, aspec = pl.BlockSpec(memory_space=VMEM), pl.BlockSpec(memory_space=ANY)
     dma = pltpu.SemaphoreType.DMA
-    flow, xr, yr = pl.pallas_call(
+    vel, st = pl.pallas_call(
         flow_kernel,
-        out_shape=[sds(896, 256), sds(2, 9, 8, 256), sds(2, 144, 256)],
+        out_shape=[sds(3, 24, 2304)] * 2,
         in_specs=[aspec] * 7,
-        out_specs=[vspec] * 3,
+        out_specs=[aspec] * 2,
         scratch_shapes=[VMEM(t.shape, bf16) for t in tb]
         + [
             VMEM((3, 24, 2304), f32), VMEM((896, 256), f32), VMEM((8, 6, 7, 8, 1, 128), f32), VMEM((3, 4, 2, 2, 7, 8, 1, 128), f32),
@@ -462,18 +493,34 @@
             VMEM((18, 192, 128), f32), VMEM((3, 4, 2, 2, 7, 8, 1, 128), f32), VMEM((8, 6, 7, 8, 1, 128), f32),
             VMEM((288, 384), f32), VMEM((192, 384), f32), VMEM((192, 384), f32),
             VMEM((2, 576, 384), f32), VMEM((2, 576, 384), f32), VMEM((256, 896), f32), VMEM((2, 9, 8, 256), f32),
-            dma((7,)), dma, dma((3,)), dma, dma((3,)), dma((2, 3, 2)), dma((2, 3)), dma((2, 4)),
+            VMEM((896, 256), f32), VMEM((2, 9, 8, 256), f32), VMEM((2, 144, 256), f32),
+            VMEM((3, 24, 2304), f32), VMEM((3, 24, 2304), f32), VMEM((896, 256), f32),
+            VMEM((36, 24, 256), f32), VMEM((36, 24, 256), f32),
+            dma((7,)), dma, dma((3,)), dma, dma((3,)), dma((2, 3, 2)), dma((2, 3)), dma((2, 4)), dma((2,)),
         ],
         compiler_params=pltpu.CompilerParams(collective_id=0, has_side_effects=True, vmem_limit_bytes=60 * 1024 * 1024),
     )(vort, *tb)
     return pl.pallas_call(
-        stretch_kernel,
-        out_shape=[sds(3, 24, 2304), sds(3, 24, 2304)],
-        in_specs=[vspec] * 4,
-        out_specs=[vspec] * 2,
-        scratch_shapes=[VMEM((36, 40, 256), f32)],
+        hand_over,
+        out_shape=[sds(3, 24, 2304)] * 2,
+        in_specs=[aspec] * 2,
+        out_specs=[aspec] * 2,
+        scratch_shapes=[VMEM((3, 24, 2304), f32), VMEM((3, 24, 2304), f32), dma((2, 2, 3))],
         compiler_params=pltpu.CompilerParams(vmem_limit_bytes=61 * 1024 * 1024),
-    )(vort, flow, xr, yr)
+    )(vel, st)
+
+
+def hand_over(vel, st, vel_o, st_o, a, b, sem):
+    triples = [(k, c, x, t, o) for k, (x, t, o) in enumerate(((vel, a, vel_o), (st, b, st_o))) for c in range(3)]
+    ins = [pltpu.make_async_copy(x.at[c], t.at[c], sem.at[0, k, c]) for k, c, x, t, o in triples]
+    outs = [pltpu.make_async_copy(t.at[c], o.at[c], sem.at[1, k, c]) for k, c, x, t, o in triples]
+    for cp in ins:
+        cp.start()
+    for i, o in zip(ins, outs):
+        i.wait()
+        o.start()
+    for cp in outs:
+        cp.wait()
 
 
 def solution(mesh):

time: 60.4 us -> 57.7 us (0.955)
  Pallas kernels: 59.6 us -> 57 us
    pallas_call x2, Pallas kernels: 59.6 us -> 57 us  [the longest x1 54.8 us: on_device(): pl.pallas_call(flow_kernel, out_shape=[sds(3, 24, 2304)] * 2, in_specs=[a...]
where the time goes in v2:
time: 57.7 us; the launch traced here: 57.6 us
  Pallas kernels  57 us (99%)
  between operations  0.64 us (1%)
    pallas_call x1, Pallas kernels, on_device(): pl.pallas_call(flow_kernel, out_shape=[sds(3, 24, 2304)] * 2, in_specs=[a...  54.8 us
    pallas_call x1, Pallas kernels, on_device(): pl.pallas_call(hand_over, out_shape=[sds(3, 24, 2304)] * 2, in_specs=[asp...  2.2 us

profile of v2, /device:TPU:1, one launch (start us, length us, event | category | flops | bytes accessed | tf_op | source)
XLA Modules:
  0.0 57.6 jit_solution(15755981193455642329)
XLA Ops:
  0.6 54.8 %shard_map.86 = (f32[3,24,2304]{2,1,0:T(8,128)}, f32[3,24,2304]{2,1,0:T(8,128)}) custom-call(f32[3,24,2304]{2,1,0:T(8,128)} %vort_h.1, bf16[2,384,256]{2,1,0:T(8,128)(2,1)} %constant.12.clone.zf_h, bf16[384,576]{1,0:T(8,128)(2,1)} %constant.13.clone.yf_h, bf16[2,2,128,384]{3,2,1,0:T(8,128)(2,1)} %constant.14.clone.xf_h, ...), custom_call_target="tpu_custom_call" | custom-call | tf_op jit(solution)/shard_map/pallas_call | solution.py:484
  55.4 2.2 %shard_map.87 = (f32[3,24,2304]{2,1,0:T(8,128)}, f32[3,24,2304]{2,1,0:T(8,128)}) custom-call(f32[3,24,2304]{2,1,0:T(8,128)} %get-tuple-element.4.vel, f32[3,24,2304]{2,1,0:T(8,128)} %get-tuple-element.5.st), custom_call_target="tpu_custom_call" | custom-call | tf_op jit(solution)/shard_map/pallas_call | solution.py:503

commit v3 on v2

--- a/solution.py
+++ b/solution.py
@@ -143,7 +143,7 @@
 B = 48
 
 
-def x_stage(g, chip, core, yt, th, xf, xi, gt, ub, uo, f, u):
+def x_stage(g, chip, core, yt, th, xf, xi, gt, ub, uo, f, u, done):
     unit = 2.0 * math.pi / N
     lane = lanes((8, 128))
     row = lax.broadcasted_iota(jnp.int32, (8, 128), 0)
@@ -184,17 +184,17 @@
         hi, lo = split(u[ib])
         back = dot(cat([hi, lo, hi], 1), ti)
         for t, c, s in combos:
-            rows = pl.ds(96 * s + B * ib, B)
             zmc = 6 * g + 3 * t + c
             r0 = at(t, c, s)
-            ub[core, zmc, rows, :] = back[r0 : r0 + B, :128]
-            uo[zmc, rows, :] = back[r0 : r0 + B, 128:]
+            ub[core, zmc, s, pl.ds(B * ib, B), :] = back[r0 : r0 + B, :128]
+            uo[zmc, s, pl.ds(B * ib, B), :] = back[r0 : r0 + B, 128:]
+        done(ib)
 
 
 def y_backward(g, h2, ub, ty, out, o):
     zm = 2 * g + h2
     lane = lanes((8, 128))
-    rhs = cat([cat([ub[h, 3 * zm + c] for c in range(3)], 1) for h in range(2)], 0)
+    rhs = cat([cat([ub[h, 3 * zm + c, i] for c in range(3)], 1) for h in range(2) for i in range(2)], 0)
     hi, lo = split(rhs)
     o[...] = dot(ty[...], cat([hi, lo, hi], 0))
     for pp in range(4):
@@ -261,8 +261,8 @@
     for i in range(36):
         top[i, pl.ds(6, 2), :] = xr[0, i // 4, pl.ds(2 * (i % 4), 2), :]
         low[i, pl.ds(10, 2), :] = xr[1, i // 4, pl.ds(2 * (i % 4), 2), :]
-    for yp in range(6):
-        for c in range(3):
+    for c in range(3):
+        for yp in range(6):
             pair = []
             for y in (2 * yp, 2 * yp + 1):
                 i = 3 * y + c
@@ -293,10 +293,10 @@
 
 def flow_kernel(
     vort_h, zf_h, yf_h, xf_h, xi_h, yi_h, zi_h,
-    vel_h, st_h,
+    vel, st,
     zf, yf, xf, xi, yi, zi, vort, w, zt, rv, yt, th, ub, uo, bk, vv, gt, s, o, f, u, acc, xs,
-    flow, xr, yr, vel, st, part, top, low,
-    tsem, fs, fr, bs, br, d1, d2, hs, os,
+    flow, xr, yr, part, top, low,
+    tsem, fs, fr, bs, br, d1, d2, hs,
 ):
     p, q = lax.axis_index("px"), lax.axis_index("py")
     core, half, qc = q % 2, p % 2, q // 2
@@ -365,22 +365,19 @@
             device_id=(p, other), device_id_type=MESH,
         )
 
-    def swap2(g):
+    def swap2(g, ib):
+        cut = lambda ref: ref.at[pl.ds(6 * g, 6), :, pl.ds(B * ib, B), :]
         return pltpu.make_async_remote_copy(
-            uo.at[pl.ds(6 * g, 6)], ub.at[core, pl.ds(6 * g, 6)], d2.at[0, g], d2.at[1, g],
-            device_id=(p, other), device_id_type=MESH,
+            cut(uo), cut(ub.at[core]), d2.at[0, g, ib], d2.at[1, g, ib], device_id=(p, other), device_id_type=MESH,
         )
 
     def arrive(g):
         t = rv.at[g]
         pltpu.make_async_copy(t, t, fr.at[g]).wait()
 
-        def one(t, _):
-            y_forward(g, t, rows_in, yf, yt, s)
+        for t in range(2):
+            y_forward(g, t, rows_in, yf, yt, s.at[t])
             swap1(g, t).start()
-            return 0
-
-        lax.fori_loop(0, 2, one, 0)
 
     for cp in loads[2:]:
         cp.wait()
@@ -389,20 +386,17 @@
     def group(g, _):
         swap1(g, 0).wait_recv()
         swap1(g, 1).wait_recv()
-        x_stage(g, chip, core, yt, th, xf, xi, gt, ub, uo, f, u)
-        swap2(g).start()
+        x_stage(g, chip, core, yt, th, xf, xi, gt, ub, uo, f, u, lambda ib: swap2(g, ib).start())
 
         @pl.when(g < 2)
         def _():
             arrive(g + 1)
 
-        swap2(g).wait_recv()
-
-        def one(t, _):
-            y_backward(g, t, ub, yi, rows_out, o)
-            return 0
-
-        lax.fori_loop(0, 2, one, 0)
+        for ib in range(2):
+            swap2(g, ib).wait_recv()
+
+        for t in range(2):
+            y_backward(g, t, ub, yi, rows_out, o.at[t])
 
         ds = vv.at[p, pl.ds(2 * g, 2), :, qc]
         for dc in (1, 0):
@@ -445,14 +439,13 @@
     for yp in range(6):
         for c in range(3):
             put(vel, c, yp, [flow[pl.ds(24 * (3 * (2 * yp + e) + c), 24), :] for e in range(2)])
-    out_vel = pltpu.make_async_copy(vel, vel_h, os.at[0])
-    out_vel.start()
     inner_stretch(flow, w, part)
 
     for g in range(3):
         swap1(g, 0).wait_send()
         swap1(g, 1).wait_send()
-        swap2(g).wait_send()
+        for ib in range(2):
+            swap2(g, ib).wait_send()
     flat = [zt.reshape(2688, 1, 128), bk.reshape(2688, 1, 128)]
     for n, cond in ((63, own), (64, jnp.logical_not(own))):
         @pl.when(cond)
@@ -468,10 +461,6 @@
             cps[back[k]].wait_recv()
 
     edge_stretch(w, part, xr, yr, top, low, st)
-    out_st = pltpu.make_async_copy(st, st_h, os.at[1])
-    out_st.start()
-    out_vel.wait()
-    out_st.wait()
 
 
 def sds(*shape):
@@ -483,42 +472,37 @@
     dma = pltpu.SemaphoreType.DMA
     vel, st = pl.pallas_call(
         flow_kernel,
-        out_shape=[sds(3, 24, 2304)] * 2,
+        out_shape=[VMEM((3, 24, 2304), f32)] * 2,
         in_specs=[aspec] * 7,
-        out_specs=[aspec] * 2,
+        out_specs=[vspec] * 2,
         scratch_shapes=[VMEM(t.shape, bf16) for t in tb]
         + [
             VMEM((3, 24, 2304), f32), VMEM((896, 256), f32), VMEM((8, 6, 7, 8, 1, 128), f32), VMEM((3, 4, 2, 2, 7, 8, 1, 128), f32),
-            VMEM((2, 18, 192, 128), f32), VMEM((18, 192, 128), f32), VMEM((2, 18, 192, 128), f32),
-            VMEM((18, 192, 128), f32), VMEM((3, 4, 2, 2, 7, 8, 1, 128), f32), VMEM((8, 6, 7, 8, 1, 128), f32),
-            VMEM((288, 384), f32), VMEM((192, 384), f32), VMEM((192, 384), f32),
+            VMEM((2, 18, 192, 128), f32), VMEM((18, 192, 128), f32), VMEM((2, 18, 2, 96, 128), f32),
+            VMEM((18, 2, 96, 128), f32), VMEM((3, 4, 2, 2, 7, 8, 1, 128), f32), VMEM((8, 6, 7, 8, 1, 128), f32),
+            VMEM((288, 384), f32), VMEM((2, 192, 384), f32), VMEM((2, 192, 384), f32),
             VMEM((2, 576, 384), f32), VMEM((2, 576, 384), f32), VMEM((256, 896), f32), VMEM((2, 9, 8, 256), f32),
             VMEM((896, 256), f32), VMEM((2, 9, 8, 256), f32), VMEM((2, 144, 256), f32),
-            VMEM((3, 24, 2304), f32), VMEM((3, 24, 2304), f32), VMEM((896, 256), f32),
+            VMEM((896, 256), f32),
             VMEM((36, 24, 256), f32), VMEM((36, 24, 256), f32),
-            dma((7,)), dma, dma((3,)), dma, dma((3,)), dma((2, 3, 2)), dma((2, 3)), dma((2, 4)), dma((2,)),
+            dma((7,)), dma, dma((3,)), dma, dma((3,)), dma((2, 3, 2)), dma((2, 3, 2)), dma((2, 4)),
         ],
-        compiler_params=pltpu.CompilerParams(collective_id=0, has_side_effects=True, vmem_limit_bytes=60 * 1024 * 1024),
+        compiler_params=pltpu.CompilerParams(collective_id=0, has_side_effects=True, vmem_limit_bytes=58 * 1024 * 1024),
     )(vort, *tb)
     return pl.pallas_call(
         hand_over,
         out_shape=[sds(3, 24, 2304)] * 2,
-        in_specs=[aspec] * 2,
+        in_specs=[vspec] * 2,
         out_specs=[aspec] * 2,
-        scratch_shapes=[VMEM((3, 24, 2304), f32), VMEM((3, 24, 2304), f32), dma((2, 2, 3))],
-        compiler_params=pltpu.CompilerParams(vmem_limit_bytes=61 * 1024 * 1024),
+        scratch_shapes=[dma((2, 3))],
+        compiler_params=pltpu.CompilerParams(vmem_limit_bytes=30 * 1024 * 1024),
     )(vel, st)
 
 
-def hand_over(vel, st, vel_o, st_o, a, b, sem):
-    triples = [(k, c, x, t, o) for k, (x, t, o) in enumerate(((vel, a, vel_o), (st, b, st_o))) for c in range(3)]
-    ins = [pltpu.make_async_copy(x.at[c], t.at[c], sem.at[0, k, c]) for k, c, x, t, o in triples]
-    outs = [pltpu.make_async_copy(t.at[c], o.at[c], sem.at[1, k, c]) for k, c, x, t, o in triples]
-    for cp in ins:
+def hand_over(vel, st, vel_o, st_o, sem):
+    outs = [pltpu.make_async_copy(x.at[c], o.at[c], sem.at[k, c]) for k, (x, o) in enumerate(((vel, vel_o), (st, st_o))) for c in range(3)]
+    for cp in outs:
         cp.start()
-    for i, o in zip(ins, outs):
-        i.wait()
-        o.start()
     for cp in outs:
         cp.wait()
 

time: 57.7 us -> 54.5 us (0.945)
  Pallas kernels: 57 us -> 53.8 us
    pallas_call x2, Pallas kernels: 57 us -> 53.8 us  [the longest x1 52.6 us: on_device(): pl.pallas_call(flow_kernel, out_shape=[VMEM((3, 24, 2304), f32)] * 2, in_...]
where the time goes in v3:
time: 54.5 us; the launch traced here: 54.4 us
  Pallas kernels  53.8 us (99%)
  between operations  0.64 us (1%)
    pallas_call x1, Pallas kernels, on_device(): pl.pallas_call(flow_kernel, out_shape=[VMEM((3, 24, 2304), f32)] * 2, in_...  52.6 us
    pallas_call x1, Pallas kernels, on_device(): pl.pallas_call(hand_over, out_shape=[sds(3, 24, 2304)] * 2, in_specs=[vsp...  1.11 us

profile of v3, /device:TPU:1, one launch (start us, length us, event | category | flops | bytes accessed | tf_op | source)
XLA Modules:
  0.0 54.4 jit_solution(9442950252939997962)
XLA Ops:
  0.6 52.6 %shard_map.86 = (f32[3,24,2304]{2,1,0:T(8,128)S(1)}, f32[3,24,2304]{2,1,0:T(8,128)S(1)}) custom-call(f32[3,24,2304]{2,1,0:T(8,128)} %vort_h.1, bf16[2,384,256]{2,1,0:T(8,128)(2,1)} %constant.12.clone.zf_h, bf16[384,576]{1,0:T(8,128)(2,1)} %constant.13.clone.yf_h, bf16[2,2,128,384]{3,2,1,0:T(8,128)(2,1)} %constant.14.clone.xf_h, ...), custom_call_target="tpu_custom_call" | custom-call | tf_op jit(solution)/shard_map/pallas_call | solution.py:473
  53.3 1.1 %shard_map.87 = (f32[3,24,2304]{2,1,0:T(8,128)}, f32[3,24,2304]{2,1,0:T(8,128)}) custom-call(f32[3,24,2304]{2,1,0:T(8,128)S(1)} %get-tuple-element.4.vel, f32[3,24,2304]{2,1,0:T(8,128)S(1)} %get-tuple-element.5.st), custom_call_target="tpu_custom_call" | custom-call | tf_op jit(solution)/shard_map/pallas_call | solution.py:492

commit v4 on v3

--- a/solution.py
+++ b/solution.py
@@ -415,10 +415,6 @@
         pltpu.make_async_copy(t, t, br.at[g]).wait()
         z_backward(g, vin, zi, acc, flow)
 
-    for m in range(9):
-        for e, r0 in ((0, 0), (1, 22)):
-            for i in range(4):
-                xs[e, m, pl.ds(2 * i, 2), :] = flow[pl.ds(24 * (4 * m + i) + r0, 2), :]
     srcs = [xs.at[0], xs.at[1], flow.at[pl.ds(0, 144)], flow.at[pl.ds(720, 144)]]
     dsts = [xr.at[1], xr.at[0], yr.at[1], yr.at[0]]
     back = [1, 0, 3, 2]
@@ -426,9 +422,19 @@
     for k, (has, dev) in enumerate(near):
         cps.append(pltpu.make_async_remote_copy(srcs[k], dsts[k], hs.at[0, k], hs.at[1, k], device_id=dev, device_id_type=MESH))
 
-        @pl.when(has)
-        def _(k=k):
+    def start(k):
+        @pl.when(near[k][0])
+        def _():
             cps[k].start()
+
+    start(2)
+    start(3)
+    for m in range(9):
+        for e, r0 in ((0, 0), (1, 22)):
+            for i in range(4):
+                xs[e, m, pl.ds(2 * i, 2), :] = flow[pl.ds(24 * (4 * m + i) + r0, 2), :]
+    start(0)
+    start(1)
 
     ends = [xr.at[0], xr.at[1], yr.at[0], yr.at[1]]
     for k, ref in enumerate(ends):

time: 54.5 us -> 54.4 us (level)
  no operation moved by 1% of the time
where the time goes in v4:
time: 54.4 us; the launch traced here: 54.3 us
  Pallas kernels  53.7 us (99%)
  between operations  0.64 us (1%)
    pallas_call x1, Pallas kernels, on_device(): pl.pallas_call(flow_kernel, out_shape=[VMEM((3, 24, 2304), f32)] * 2, in_...  52.6 us
    pallas_call x1, Pallas kernels, on_device(): pl.pallas_call(hand_over, out_shape=[sds(3, 24, 2304)] * 2, in_specs=[vsp...  1.11 us

profile of v4, /device:TPU:1, one launch (start us, length us, event | category | flops | bytes accessed | tf_op | source)
XLA Modules:
  0.0 54.3 jit_solution(4379423345904487637)
XLA Ops:
  0.6 52.6 %shard_map.86 = (f32[3,24,2304]{2,1,0:T(8,128)S(1)}, f32[3,24,2304]{2,1,0:T(8,128)S(1)}) custom-call(f32[3,24,2304]{2,1,0:T(8,128)} %vort_h.1, bf16[2,384,256]{2,1,0:T(8,128)(2,1)} %constant.12.clone.zf_h, bf16[384,576]{1,0:T(8,128)(2,1)} %constant.13.clone.yf_h, bf16[2,2,128,384]{3,2,1,0:T(8,128)(2,1)} %constant.14.clone.xf_h, ...), custom_call_target="tpu_custom_call" | custom-call | tf_op jit(solution)/shard_map/pallas_call | solution.py:479
  53.2 1.1 %shard_map.87 = (f32[3,24,2304]{2,1,0:T(8,128)}, f32[3,24,2304]{2,1,0:T(8,128)}) custom-call(f32[3,24,2304]{2,1,0:T(8,128)S(1)} %get-tuple-element.4.vel, f32[3,24,2304]{2,1,0:T(8,128)S(1)} %get-tuple-element.5.st), custom_call_target="tpu_custom_call" | custom-call | tf_op jit(solution)/shard_map/pallas_call | solution.py:498
